TPU v7x, 512 devices: a whole 4x8x8 slice. The times are simulated.
512 devices in a mesh: sector: 64 (over x, z_lo, y), block: 8 (over z_hi, core).
Axes of the slice: x: 4, y: 8, z: 8 (z_hi: 4, z_lo: 2; z = z_hi * 2 + z_lo), core: 2. Of those that a mesh axis runs over, the one named last changes fastest.
Arguments:
- adjoint_prev: float32 [5, 64, 512, 128], P(None, 'block', 'sector'), may hold values from -6 to 6
- adjoint_source: float32 [5, 64, 512, 128], P(None, 'block', 'sector'), may hold values from -6 to 6
- face_matrices: bfloat16 [3, 5, 5, 64, 512, 128], P(None, None, None, 'block', 'sector'), may hold values from -2.5 to 2.5
- inverse_blocks: bfloat16 [5, 5, 64, 512, 128], P(None, None, 'block', 'sector')
- sector_offset: int32 [1], replicated, may hold values from 1 to 63
- donor_cells: int32 [512], P('sector'), may hold values from 0 to 7
- donor_weights: float32 [512], P('sector'), may hold values from 0.1 to 0.9
Outputs:
- adjoint: float32 [5, 64, 512, 128], P(None, 'block', 'sector')
- last_update: float32 [5, 64, 512, 128], P(None, 'block', 'sector')
All inputs are finite; a program needn't handle non-finite values.
Results may differ from a plain program's by a relative error of at most 0.0003.
Values sent between devices are 32-bit elements; how exact they have to be, the bound alone decides.
A program may use at most 64 MiB of HBM per device.

v0:
```python
import jax
import jax.numpy as jnp
from jax import lax
from jax.sharding import PartitionSpec as P

ITERS = 4


def passed_along(value, axis, steps):
    count = lax.axis_size(axis)
    pairs = [(source, (source + steps) % count) for source in range(count)]
    return lax.ppermute(value, axis, pairs)


def padded(cells, sides, width, closed):
    for axis, dim in sides:
        count = lax.axis_size(axis)
        ends = count if closed else count - 1
        head = lax.slice_in_dim(cells, 0, width, axis=dim)
        tail = lax.slice_in_dim(cells, cells.shape[dim] - width, cells.shape[dim], axis=dim)
        cells = jnp.concatenate(
            [
                lax.ppermute(tail, axis, [(i, (i + 1) % count) for i in range(ends)]),
                cells,
                lax.ppermute(head, axis, [((i + 1) % count, i) for i in range(ends)]),
            ],
            axis=dim,
        )
    return cells


def shards(
    adjoint_prev,
    adjoint_source,
    face_matrices,
    inverse_blocks,
    sector_offset,
    donor_cells,
    donor_weights,
):
    sectors = lax.axis_size("sector")
    blocks = lax.axis_size("block")
    block_index = lax.axis_index("block")
    cells_around = adjoint_prev.shape[2]
    offset_value = sector_offset[0]
    columns = jnp.arange(cells_around + 1, dtype=jnp.int32)
    first_hit = (columns[None, :] == donor_cells[:, None]).astype(jnp.float32)
    second_hit = (columns[None, :] == donor_cells[:, None] + 1).astype(jnp.float32)
    blend_table = donor_weights[:, None] * first_hit + (1.0 - donor_weights[:, None]) * second_hit
    adjoint = adjoint_prev
    last_update = jnp.zeros_like(adjoint_prev)
    for sweep_number in range(ITERS):
        beside_all = padded(adjoint, (("sector", 2),), 1, True)
        along = padded(adjoint, (("block", 1),), 1, False)
        sweep_lower_rim = along[:, 0]
        upper_rim = along[:, -1]
        around_minus = beside_all[:, :, :-2]
        around_plus = beside_all[:, :, 2:]
        following = passed_along(sweep_lower_rim[:, :1], "sector", -1)
        extended = jnp.concatenate([sweep_lower_rim, following], axis=1)
        moved_rows = extended
        for bit_number in range((sectors - 1).bit_length()):
            hopped = passed_along(moved_rows, "sector", 1 << bit_number)
            moved_rows = jnp.where(offset_value >> bit_number & 1 == 1, hopped, moved_rows)
        facing = jnp.einsum("jk,nkr->njr", blend_table, moved_rows, precision=lax.Precision.HIGHEST)
        sweep_lower_rim = jnp.where(block_index == blocks // 2, facing, sweep_lower_rim)
        axial_minus = jnp.concatenate([sweep_lower_rim[:, None], adjoint[:, :-1]], axis=1)
        axial_plus = jnp.concatenate([adjoint[:, 1:], upper_rim[:, None]], axis=1)
        radial_pad = jnp.pad(adjoint, ((0, 0), (0, 0), (0, 0), (1, 1)))
        mixed = (
            0.6 * axial_minus + 0.4 * axial_plus,
            0.6 * around_minus + 0.4 * around_plus,
            0.6 * radial_pad[:, :, :, :-2] + 0.4 * radial_pad[:, :, :, 2:],
        )
        coupled = jnp.zeros_like(adjoint)
        for direction in range(3):
            for comp in range(5):
                coupled = (
                    coupled
                    + face_matrices[direction, comp].astype(jnp.float32)
                    * mixed[direction][comp][None]
                )
        total = adjoint_source + coupled
        result = jnp.zeros_like(adjoint)
        for comp in range(5):
            result = result + inverse_blocks[:, comp].astype(jnp.float32) * total[comp][None]
        last_update = result - adjoint
        adjoint = result
    return (adjoint, last_update)


def solution(mesh):
    return jax.shard_map(
        shards,
        mesh=mesh,
        in_specs=(
            P(None, "block", "sector", None),
            P(None, "block", "sector", None),
            P(None, None, None, "block", "sector", None),
            P(None, None, "block", "sector", None),
            P(),
            P("sector"),
            P("sector"),
        ),
        out_specs=(P(None, "block", "sector", None), P(None, "block", "sector", None)),
        check_vma=False,
    )
```

profile of v0, /device:TPU:256, one launch (start us, length us, event | category | flops | bytes accessed | tf_op | source)
XLA Modules:
  0.0 296.3 jit_solution(5195664377136242498)
XLA Ops:
  3.4 5.8 %collective-permute-start.8 = (f32[5,1,8,128]{3,2,0,1:T(8,128)S(1)}, f32[5,1,8,128]{3,2,0,1:T(8,128)S(1)}, u32[]{:S(2)}, u32[]{:S(2)}) collective-permute-start(f32[5,1,8,128]{3,2,0,1:T(8,128)S(1)} %get-tuple-element.107), channel_id=1, source_target_pairs={{1,0},{2,1},{3,2},{4,3},{5,4},{6,5},{7,6},{9,8},{10,9},{11,10},{12... | collective-permute-start | bytes 61448 | tf_op jit(solution)/shard_map/ppermute | solution.py:25
  9.1 8.5 %collective-permute-start.1 = (f32[5,1,128]{2,1,0:T(1,128)S(1)}, f32[5,1,128]{2,1,0:T(1,128)S(1)}, u32[]{:S(2)}, u32[]{:S(2)}) collective-permute-start(f32[5,1,128]{2,1,0:T(1,128)S(1)} %slice.645), channel_id=1, source_target_pairs={{0,504},{8,0},{16,8},{24,16},{32,24},{40,32},{48,40},{56,48},{64,5... | collective-permute-start | bytes 7688 | tf_op jit(solution)/shard_map/ppermute | solution.py:12
  28.1 6.5 %collective-permute-done.2 = f32[5,9,128]{2,1,0:T(8,128)S(1)} collective-permute-done((f32[5,9,128]{2,1,0:T(8,128)S(1)}, f32[5,9,128]{2,1,0:T(8,128)S(1)}, u32[]{:S(2)}, u32[]{:S(2)}) %collective-permute-start.2) | collective-permute-done | bytes 23072 | tf_op jit(solution)/shard_map/ppermute | solution.py:12
  37.7 8.0 %collective-permute-done.3 = f32[5,9,128]{2,1,0:T(8,128)S(1)} collective-permute-done((f32[5,9,128]{2,1,0:T(8,128)S(1)}, f32[5,9,128]{2,1,0:T(8,128)S(1)}, u32[]{:S(2)}, u32[]{:S(2)}) %collective-permute-start.3) | collective-permute-done | bytes 23072 | tf_op jit(solution)/shard_map/ppermute | solution.py:12
  47.6 10.9 %collective-permute-done.4 = f32[5,9,128]{2,1,0:T(8,128)S(1)} collective-permute-done((f32[5,9,128]{2,1,0:T(8,128)S(1)}, f32[5,9,128]{2,1,0:T(8,128)S(1)}, u32[]{:S(2)}, u32[]{:S(2)}) %collective-permute-start.4) | collective-permute-done | bytes 23072 | tf_op jit(solution)/shard_map/ppermute | solution.py:12
  60.4 6.0 %collective-permute-done.5 = f32[5,9,128]{2,1,0:T(8,128)S(1)} collective-permute-done((f32[5,9,128]{2,1,0:T(8,128)S(1)}, f32[5,9,128]{2,1,0:T(8,128)S(1)}, u32[]{:S(2)}, u32[]{:S(2)}) %collective-permute-start.5) | collective-permute-done | bytes 23072 | tf_op jit(solution)/shard_map/ppermute | solution.py:12
  68.8 5.0 %collective-permute-done.6 = f32[5,9,128]{2,1,0:T(8,128)S(1)} collective-permute-done((f32[5,9,128]{2,1,0:T(8,128)S(1)}, f32[5,9,128]{2,1,0:T(8,128)S(1)}, u32[]{:S(2)}, u32[]{:S(2)}) %collective-permute-start.6) | collective-permute-done | bytes 23072 | tf_op jit(solution)/shard_map/ppermute | solution.py:12
  75.7 5.4 %collective-permute-done.7 = f32[5,9,128]{2,1,0:T(8,128)S(1)} collective-permute-done((f32[5,9,128]{2,1,0:T(8,128)S(1)}, f32[5,9,128]{2,1,0:T(8,128)S(1)}, u32[]{:S(2)}, u32[]{:S(2)}) %collective-permute-start.7) | collective-permute-done | bytes 23072 | tf_op jit(solution)/shard_map/ppermute | solution.py:12
  83.8 5.3 %collective-permute-done.11 = f32[5,1,8,128]{3,2,0,1:T(8,128)S(1)} collective-permute-done((f32[5,1,8,128]{3,2,0,1:T(8,128)S(1)}, f32[5,1,8,128]{3,2,0,1:T(8,128)S(1)}, u32[]{:S(2)}, u32[]{:S(2)}) %collective-permute-start.11) | collective-permute-done | bytes 20512 | tf_op jit(solution)/shard_map/ppermute | solution.py:23
  91.0 3.6 %collective-permute-done.12 = f32[5,1,128]{2,1,0:T(1,128)S(1)} collective-permute-done((f32[5,1,128]{2,1,0:T(1,128)S(1)}, f32[5,1,128]{2,1,0:T(1,128)S(1)}, u32[]{:S(2)}, u32[]{:S(2)}) %collective-permute-start.12) | collective-permute-done | bytes 2592 | tf_op jit(solution)/shard_map/ppermute | solution.py:12
  96.5 8.2 %collective-permute-done.13 = f32[5,9,128]{2,1,0:T(8,128)S(1)} collective-permute-done((f32[5,9,128]{2,1,0:T(8,128)S(1)}, f32[5,9,128]{2,1,0:T(8,128)S(1)}, u32[]{:S(2)}, u32[]{:S(2)}) %collective-permute-start.13) | collective-permute-done | bytes 23072 | tf_op jit(solution)/shard_map/ppermute | solution.py:12
  106.6 9.1 %collective-permute-done.14 = f32[5,9,128]{2,1,0:T(8,128)S(1)} collective-permute-done((f32[5,9,128]{2,1,0:T(8,128)S(1)}, f32[5,9,128]{2,1,0:T(8,128)S(1)}, u32[]{:S(2)}, u32[]{:S(2)}) %collective-permute-start.14) | collective-permute-done | bytes 23072 | tf_op jit(solution)/shard_map/ppermute | solution.py:12
  121.5 8.1 %collective-permute-start.21 = (f32[5,8,1,128]{3,2,0,1:T(1,128)S(1)}, f32[5,8,1,128]{3,2,0,1:T(1,128)S(1)}, u32[]{:S(2)}, u32[]{:S(2)}) collective-permute-start(f32[5,8,1,128]{3,2,0,1:T(1,128)S(1)} %get-tuple-element.89), channel_id=1, source_target_pairs={{8,0},{16,8},{24,16},{32,24},{40,32},{48,40},{56,48},{64,56},{72,6... | collective-permute-start | bytes 61448 | tf_op jit(solution)/shard_map/ppermute | solution.py:25
  131.8 5.9 %collective-permute-done.16 = f32[5,9,128]{2,1,0:T(8,128)S(1)} collective-permute-done((f32[5,9,128]{2,1,0:T(8,128)S(1)}, f32[5,9,128]{2,1,0:T(8,128)S(1)}, u32[]{:S(2)}, u32[]{:S(2)}) %collective-permute-start.16) | collective-permute-done | bytes 23072 | tf_op jit(solution)/shard_map/ppermute | solution.py:12
  139.6 5.2 %collective-permute-done.17 = f32[5,9,128]{2,1,0:T(8,128)S(1)} collective-permute-done((f32[5,9,128]{2,1,0:T(8,128)S(1)}, f32[5,9,128]{2,1,0:T(8,128)S(1)}, u32[]{:S(2)}, u32[]{:S(2)}) %collective-permute-start.17) | collective-permute-done | bytes 23072 | tf_op jit(solution)/shard_map/ppermute | solution.py:12
  146.7 5.4 %collective-permute-done.18 = f32[5,9,128]{2,1,0:T(8,128)S(1)} collective-permute-done((f32[5,9,128]{2,1,0:T(8,128)S(1)}, f32[5,9,128]{2,1,0:T(8,128)S(1)}, u32[]{:S(2)}, u32[]{:S(2)}) %collective-permute-start.18) | collective-permute-done | bytes 23072 | tf_op jit(solution)/shard_map/ppermute | solution.py:12
  154.8 5.3 %collective-permute-done.22 = f32[5,1,8,128]{3,2,0,1:T(8,128)S(1)} collective-permute-done((f32[5,1,8,128]{3,2,0,1:T(8,128)S(1)}, f32[5,1,8,128]{3,2,0,1:T(8,128)S(1)}, u32[]{:S(2)}, u32[]{:S(2)}) %collective-permute-start.22) | collective-permute-done | bytes 20512 | tf_op jit(solution)/shard_map/ppermute | solution.py:23
  162.0 3.6 %collective-permute-done.23 = f32[5,1,128]{2,1,0:T(1,128)S(1)} collective-permute-done((f32[5,1,128]{2,1,0:T(1,128)S(1)}, f32[5,1,128]{2,1,0:T(1,128)S(1)}, u32[]{:S(2)}, u32[]{:S(2)}) %collective-permute-start.23) | collective-permute-done | bytes 2592 | tf_op jit(solution)/shard_map/ppermute | solution.py:12
  167.5 8.2 %collective-permute-done.24 = f32[5,9,128]{2,1,0:T(8,128)S(1)} collective-permute-done((f32[5,9,128]{2,1,0:T(8,128)S(1)}, f32[5,9,128]{2,1,0:T(8,128)S(1)}, u32[]{:S(2)}, u32[]{:S(2)}) %collective-permute-start.24) | collective-permute-done | bytes 23072 | tf_op jit(solution)/shard_map/ppermute | solution.py:12
  177.7 9.1 %collective-permute-done.25 = f32[5,9,128]{2,1,0:T(8,128)S(1)} collective-permute-done((f32[5,9,128]{2,1,0:T(8,128)S(1)}, f32[5,9,128]{2,1,0:T(8,128)S(1)}, u32[]{:S(2)}, u32[]{:S(2)}) %collective-permute-start.25) | collective-permute-done | bytes 23072 | tf_op jit(solution)/shard_map/ppermute | solution.py:12
  192.5 8.1 %collective-permute-start.32 = (f32[5,8,1,128]{3,2,0,1:T(1,128)S(1)}, f32[5,8,1,128]{3,2,0,1:T(1,128)S(1)}, u32[]{:S(2)}, u32[]{:S(2)}) collective-permute-start(f32[5,8,1,128]{3,2,0,1:T(1,128)S(1)} %get-tuple-element.61), channel_id=1, source_target_pairs={{8,0},{16,8},{24,16},{32,24},{40,32},{48,40},{56,48},{64,56},{72,6... | collective-permute-start | bytes 61448 | tf_op jit(solution)/shard_map/ppermute | solution.py:25
  202.8 5.9 %collective-permute-done.27 = f32[5,9,128]{2,1,0:T(8,128)S(1)} collective-permute-done((f32[5,9,128]{2,1,0:T(8,128)S(1)}, f32[5,9,128]{2,1,0:T(8,128)S(1)}, u32[]{:S(2)}, u32[]{:S(2)}) %collective-permute-start.27) | collective-permute-done | bytes 23072 | tf_op jit(solution)/shard_map/ppermute | solution.py:12
  210.7 5.2 %collective-permute-done.28 = f32[5,9,128]{2,1,0:T(8,128)S(1)} collective-permute-done((f32[5,9,128]{2,1,0:T(8,128)S(1)}, f32[5,9,128]{2,1,0:T(8,128)S(1)}, u32[]{:S(2)}, u32[]{:S(2)}) %collective-permute-start.28) | collective-permute-done | bytes 23072 | tf_op jit(solution)/shard_map/ppermute | solution.py:12
  217.8 5.4 %collective-permute-done.29 = f32[5,9,128]{2,1,0:T(8,128)S(1)} collective-permute-done((f32[5,9,128]{2,1,0:T(8,128)S(1)}, f32[5,9,128]{2,1,0:T(8,128)S(1)}, u32[]{:S(2)}, u32[]{:S(2)}) %collective-permute-start.29) | collective-permute-done | bytes 23072 | tf_op jit(solution)/shard_map/ppermute | solution.py:12
  225.8 5.3 %collective-permute-done.33 = f32[5,1,8,128]{3,2,0,1:T(8,128)S(1)} collective-permute-done((f32[5,1,8,128]{3,2,0,1:T(8,128)S(1)}, f32[5,1,8,128]{3,2,0,1:T(8,128)S(1)}, u32[]{:S(2)}, u32[]{:S(2)}) %collective-permute-start.33) | collective-permute-done | bytes 20512 | tf_op jit(solution)/shard_map/ppermute | solution.py:23
  233.1 3.6 %collective-permute-done.34 = f32[5,1,128]{2,1,0:T(1,128)S(1)} collective-permute-done((f32[5,1,128]{2,1,0:T(1,128)S(1)}, f32[5,1,128]{2,1,0:T(1,128)S(1)}, u32[]{:S(2)}, u32[]{:S(2)}) %collective-permute-start.34) | collective-permute-done | bytes 2592 | tf_op jit(solution)/shard_map/ppermute | solution.py:12
  238.5 8.2 %collective-permute-done.35 = f32[5,9,128]{2,1,0:T(8,128)S(1)} collective-permute-done((f32[5,9,128]{2,1,0:T(8,128)S(1)}, f32[5,9,128]{2,1,0:T(8,128)S(1)}, u32[]{:S(2)}, u32[]{:S(2)}) %collective-permute-start.35) | collective-permute-done | bytes 23072 | tf_op jit(solution)/shard_map/ppermute | solution.py:12
  248.7 9.1 %collective-permute-done.36 = f32[5,9,128]{2,1,0:T(8,128)S(1)} collective-permute-done((f32[5,9,128]{2,1,0:T(8,128)S(1)}, f32[5,9,128]{2,1,0:T(8,128)S(1)}, u32[]{:S(2)}, u32[]{:S(2)}) %collective-permute-start.36) | collective-permute-done | bytes 23072 | tf_op jit(solution)/shard_map/ppermute | solution.py:12
  263.6 8.1 %collective-permute-start.43 = (f32[5,8,1,128]{3,2,0,1:T(1,128)S(1)}, f32[5,8,1,128]{3,2,0,1:T(1,128)S(1)}, u32[]{:S(2)}, u32[]{:S(2)}) collective-permute-start(f32[5,8,1,128]{3,2,0,1:T(1,128)S(1)} %get-tuple-element.33), channel_id=1, source_target_pairs={{8,0},{16,8},{24,16},{32,24},{40,32},{48,40},{56,48},{64,56},{72,6... | collective-permute-start | bytes 61448 | tf_op jit(solution)/shard_map/ppermute | solution.py:25
  273.9 5.9 %collective-permute-done.38 = f32[5,9,128]{2,1,0:T(8,128)S(1)} collective-permute-done((f32[5,9,128]{2,1,0:T(8,128)S(1)}, f32[5,9,128]{2,1,0:T(8,128)S(1)}, u32[]{:S(2)}, u32[]{:S(2)}) %collective-permute-start.38) | collective-permute-done | bytes 23072 | tf_op jit(solution)/shard_map/ppermute | solution.py:12
  281.7 5.2 %collective-permute-done.39 = f32[5,9,128]{2,1,0:T(8,128)S(1)} collective-permute-done((f32[5,9,128]{2,1,0:T(8,128)S(1)}, f32[5,9,128]{2,1,0:T(8,128)S(1)}, u32[]{:S(2)}, u32[]{:S(2)}) %collective-permute-start.39) | collective-permute-done | bytes 23072 | tf_op jit(solution)/shard_map/ppermute | solution.py:12
  288.8 5.4 %collective-permute-done.40 = f32[5,9,128]{2,1,0:T(8,128)S(1)} collective-permute-done((f32[5,9,128]{2,1,0:T(8,128)S(1)}, f32[5,9,128]{2,1,0:T(8,128)S(1)}, u32[]{:S(2)}, u32[]{:S(2)}) %collective-permute-start.40) | collective-permute-done | bytes 23072 | tf_op jit(solution)/shard_map/ppermute | solution.py:12
  (146 shorter events, 85.9 us)
Async XLA Ops:
  1.4 7.7 %collective-permute-start = (f32[5,1,8,128]{3,2,0,1:T(8,128)S(1)}, f32[5,1,8,128]{3,2,0,1:T(8,128)S(1)}, u32[]{:S(2)}, u32[]{:S(2)}) collective-permute-start(f32[5,1,8,128]{3,2,0,1:T(8,128)S(1)} %get-tuple-element.108), channel_id=1, source_target_pairs={{0,1},{1,2},{2,3},{3,4},{4,5},{5,6},{6,7},{8,9},{9,10},{10,11},{11... | collective-permute-start | bytes 61448 | tf_op jit(solution)/shard_map/ppermute | solution.py:23
  3.4 78.0 %collective-permute-start.8 = (f32[5,1,8,128]{3,2,0,1:T(8,128)S(1)}, f32[5,1,8,128]{3,2,0,1:T(8,128)S(1)}, u32[]{:S(2)}, u32[]{:S(2)}) collective-permute-start(f32[5,1,8,128]{3,2,0,1:T(8,128)S(1)} %get-tuple-element.107), channel_id=1, source_target_pairs={{1,0},{2,1},{3,2},{4,3},{5,4},{6,5},{7,6},{9,8},{10,9},{11,10},{12... | collective-permute-start | bytes 61448 | tf_op jit(solution)/shard_map/ppermute | solution.py:25
  9.1 15.4 %collective-permute-start.1 = (f32[5,1,128]{2,1,0:T(1,128)S(1)}, f32[5,1,128]{2,1,0:T(1,128)S(1)}, u32[]{:S(2)}, u32[]{:S(2)}) collective-permute-start(f32[5,1,128]{2,1,0:T(1,128)S(1)} %slice.645), channel_id=1, source_target_pairs={{0,504},{8,0},{16,8},{24,16},{32,24},{40,32},{48,40},{56,48},{64,5... | collective-permute-start | bytes 7688 | tf_op jit(solution)/shard_map/ppermute | solution.py:12
  18.7 49.9 %collective-permute-start.10 = (f32[5,8,1,128]{3,2,0,1:T(1,128)S(1)}, f32[5,8,1,128]{3,2,0,1:T(1,128)S(1)}, u32[]{:S(2)}, u32[]{:S(2)}) collective-permute-start(f32[5,8,1,128]{3,2,0,1:T(1,128)S(1)} %get-tuple-element.117), channel_id=1, source_target_pairs={{8,0},{16,8},{24,16},{32,24},{40,32},{48,40},{56,48},{64,56},{72,6... | collective-permute-start | bytes 61448 | tf_op jit(solution)/shard_map/ppermute | solution.py:25
  21.9 46.7 %collective-permute-start.9 = (f32[5,8,1,128]{3,2,0,1:T(1,128)S(1)}, f32[5,8,1,128]{3,2,0,1:T(1,128)S(1)}, u32[]{:S(2)}, u32[]{:S(2)}) collective-permute-start(f32[5,8,1,128]{3,2,0,1:T(1,128)S(1)} %get-tuple-element.116), channel_id=1, source_target_pairs={{0,8},{8,16},{16,24},{24,32},{32,40},{40,48},{48,56},{56,64},{64,7... | collective-permute-start | bytes 61448 | tf_op jit(solution)/shard_map/ppermute | solution.py:23
  24.5 10.1 %collective-permute-start.2 = (f32[5,9,128]{2,1,0:T(8,128)S(1)}, f32[5,9,128]{2,1,0:T(8,128)S(1)}, u32[]{:S(2)}, u32[]{:S(2)}) collective-permute-start(f32[5,9,128]{2,1,0:T(8,128)S(1)} %pad_maximum_fusion.8), channel_id=1, source_target_pairs={{0,8},{8,16},{16,24},{24,32},{32,40},{40,48},{48,56},{56,64},{64,7... | collective-permute-start | bytes 69128 | tf_op jit(solution)/shard_map/ppermute | solution.py:12
  34.7 11.0 %collective-permute-start.3 = (f32[5,9,128]{2,1,0:T(8,128)S(1)}, f32[5,9,128]{2,1,0:T(8,128)S(1)}, u32[]{:S(2)}, u32[]{:S(2)}) collective-permute-start(f32[5,9,128]{2,1,0:T(8,128)S(1)} %broadcast_select_fusion.3), channel_id=1, source_target_pairs={{0,16},{8,24},{16,32},{24,40},{32,48},{40,56},{48,64},{56,72},{64,... | collective-permute-start | bytes 69128 | tf_op jit(solution)/shard_map/ppermute | solution.py:12
  45.7 12.8 %collective-permute-start.4 = (f32[5,9,128]{2,1,0:T(8,128)S(1)}, f32[5,9,128]{2,1,0:T(8,128)S(1)}, u32[]{:S(2)}, u32[]{:S(2)}) collective-permute-start(f32[5,9,128]{2,1,0:T(8,128)S(1)} %broadcast_select_fusion.7), channel_id=1, source_target_pairs={{0,32},{8,40},{16,48},{24,56},{32,64},{40,72},{48,80},{56,88},{64,... | collective-permute-start | bytes 69128 | tf_op jit(solution)/shard_map/ppermute | solution.py:12
  58.5 8.0 %collective-permute-start.5 = (f32[5,9,128]{2,1,0:T(8,128)S(1)}, f32[5,9,128]{2,1,0:T(8,128)S(1)}, u32[]{:S(2)}, u32[]{:S(2)}) collective-permute-start(f32[5,9,128]{2,1,0:T(8,128)S(1)} %broadcast_select_fusion.11), channel_id=1, source_target_pairs={{0,64},{8,72},{16,80},{24,88},{32,96},{40,104},{48,112},{56,120},{... | collective-permute-start | bytes 69128 | tf_op jit(solution)/shard_map/ppermute | solution.py:12
  73.8 7.4 %collective-permute-start.7 = (f32[5,9,128]{2,1,0:T(8,128)S(1)}, f32[5,9,128]{2,1,0:T(8,128)S(1)}, u32[]{:S(2)}, u32[]{:S(2)}) collective-permute-start(f32[5,9,128]{2,1,0:T(8,128)S(1)} %broadcast_select_fusion.19), channel_id=1, source_target_pairs={{0,256},{8,264},{16,272},{24,280},{32,288},{40,296},{48,304},{56,3... | collective-permute-start | bytes 69128 | tf_op jit(solution)/shard_map/ppermute | solution.py:12
  94.6 10.1 %collective-permute-start.13 = (f32[5,9,128]{2,1,0:T(8,128)S(1)}, f32[5,9,128]{2,1,0:T(8,128)S(1)}, u32[]{:S(2)}, u32[]{:S(2)}) collective-permute-start(f32[5,9,128]{2,1,0:T(8,128)S(1)} %pad_maximum_fusion.9), channel_id=1, source_target_pairs={{0,8},{8,16},{16,24},{24,32},{32,40},{40,48},{48,56},{56,64},{64,7... | collective-permute-start | bytes 69128 | tf_op jit(solution)/shard_map/ppermute | solution.py:12
  104.7 11.0 %collective-permute-start.14 = (f32[5,9,128]{2,1,0:T(8,128)S(1)}, f32[5,9,128]{2,1,0:T(8,128)S(1)}, u32[]{:S(2)}, u32[]{:S(2)}) collective-permute-start(f32[5,9,128]{2,1,0:T(8,128)S(1)} %broadcast_select_fusion.2), channel_id=1, source_target_pairs={{0,16},{8,24},{16,32},{24,40},{32,48},{40,56},{48,64},{56,72},{64,... | collective-permute-start | bytes 69128 | tf_op jit(solution)/shard_map/ppermute | solution.py:12
  115.7 14.0 %collective-permute-start.15 = (f32[5,9,128]{2,1,0:T(8,128)S(1)}, f32[5,9,128]{2,1,0:T(8,128)S(1)}, u32[]{:S(2)}, u32[]{:S(2)}) collective-permute-start(f32[5,9,128]{2,1,0:T(8,128)S(1)} %broadcast_select_fusion.6), channel_id=1, source_target_pairs={{0,32},{8,40},{16,48},{24,56},{32,64},{40,72},{48,80},{56,88},{64,... | collective-permute-start | bytes 69128 | tf_op jit(solution)/shard_map/ppermute | solution.py:12
  117.7 34.8 %collective-permute-start.19 = (f32[5,1,8,128]{3,2,0,1:T(8,128)S(1)}, f32[5,1,8,128]{3,2,0,1:T(8,128)S(1)}, u32[]{:S(2)}, u32[]{:S(2)}) collective-permute-start(f32[5,1,8,128]{3,2,0,1:T(8,128)S(1)} %get-tuple-element.79), channel_id=1, source_target_pairs={{1,0},{2,1},{3,2},{4,3},{5,4},{6,5},{7,6},{9,8},{10,9},{11,10},{12... | collective-permute-start | bytes 61448 | tf_op jit(solution)/shard_map/ppermute | solution.py:25
  119.6 12.0 %collective-permute-start.20 = (f32[5,8,1,128]{3,2,0,1:T(1,128)S(1)}, f32[5,8,1,128]{3,2,0,1:T(1,128)S(1)}, u32[]{:S(2)}, u32[]{:S(2)}) collective-permute-start(f32[5,8,1,128]{3,2,0,1:T(1,128)S(1)} %get-tuple-element.88), channel_id=1, source_target_pairs={{0,8},{8,16},{16,24},{24,32},{32,40},{40,48},{48,56},{56,64},{64,7... | collective-permute-start | bytes 61448 | tf_op jit(solution)/shard_map/ppermute | solution.py:23
  121.5 10.1 %collective-permute-start.21 = (f32[5,8,1,128]{3,2,0,1:T(1,128)S(1)}, f32[5,8,1,128]{3,2,0,1:T(1,128)S(1)}, u32[]{:S(2)}, u32[]{:S(2)}) collective-permute-start(f32[5,8,1,128]{3,2,0,1:T(1,128)S(1)} %get-tuple-element.89), channel_id=1, source_target_pairs={{8,0},{16,8},{24,16},{32,24},{40,32},{48,40},{56,48},{64,56},{72,6... | collective-permute-start | bytes 61448 | tf_op jit(solution)/shard_map/ppermute | solution.py:25
  129.7 8.0 %collective-permute-start.16 = (f32[5,9,128]{2,1,0:T(8,128)S(1)}, f32[5,9,128]{2,1,0:T(8,128)S(1)}, u32[]{:S(2)}, u32[]{:S(2)}) collective-permute-start(f32[5,9,128]{2,1,0:T(8,128)S(1)} %broadcast_select_fusion.10), channel_id=1, source_target_pairs={{0,64},{8,72},{16,80},{24,88},{32,96},{40,104},{48,112},{56,120},{... | collective-permute-start | bytes 69128 | tf_op jit(solution)/shard_map/ppermute | solution.py:12
  144.8 7.4 %collective-permute-start.18 = (f32[5,9,128]{2,1,0:T(8,128)S(1)}, f32[5,9,128]{2,1,0:T(8,128)S(1)}, u32[]{:S(2)}, u32[]{:S(2)}) collective-permute-start(f32[5,9,128]{2,1,0:T(8,128)S(1)} %broadcast_select_fusion.18), channel_id=1, source_target_pairs={{0,256},{8,264},{16,272},{24,280},{32,288},{40,296},{48,304},{56,3... | collective-permute-start | bytes 69128 | tf_op jit(solution)/shard_map/ppermute | solution.py:12
  165.6 10.1 %collective-permute-start.24 = (f32[5,9,128]{2,1,0:T(8,128)S(1)}, f32[5,9,128]{2,1,0:T(8,128)S(1)}, u32[]{:S(2)}, u32[]{:S(2)}) collective-permute-start(f32[5,9,128]{2,1,0:T(8,128)S(1)} %pad_maximum_fusion.10), channel_id=1, source_target_pairs={{0,8},{8,16},{16,24},{24,32},{32,40},{40,48},{48,56},{56,64},{64,7... | collective-permute-start | bytes 69128 | tf_op jit(solution)/shard_map/ppermute | solution.py:12
  175.7 11.0 %collective-permute-start.25 = (f32[5,9,128]{2,1,0:T(8,128)S(1)}, f32[5,9,128]{2,1,0:T(8,128)S(1)}, u32[]{:S(2)}, u32[]{:S(2)}) collective-permute-start(f32[5,9,128]{2,1,0:T(8,128)S(1)} %broadcast_select_fusion.1), channel_id=1, source_target_pairs={{0,16},{8,24},{16,32},{24,40},{32,48},{40,56},{48,64},{56,72},{64,... | collective-permute-start | bytes 69128 | tf_op jit(solution)/shard_map/ppermute | solution.py:12
  186.7 14.0 %collective-permute-start.26 = (f32[5,9,128]{2,1,0:T(8,128)S(1)}, f32[5,9,128]{2,1,0:T(8,128)S(1)}, u32[]{:S(2)}, u32[]{:S(2)}) collective-permute-start(f32[5,9,128]{2,1,0:T(8,128)S(1)} %broadcast_select_fusion.5), channel_id=1, source_target_pairs={{0,32},{8,40},{16,48},{24,56},{32,64},{40,72},{48,80},{56,88},{64,... | collective-permute-start | bytes 69128 | tf_op jit(solution)/shard_map/ppermute | solution.py:12
  188.7 34.8 %collective-permute-start.30 = (f32[5,1,8,128]{3,2,0,1:T(8,128)S(1)}, f32[5,1,8,128]{3,2,0,1:T(8,128)S(1)}, u32[]{:S(2)}, u32[]{:S(2)}) collective-permute-start(f32[5,1,8,128]{3,2,0,1:T(8,128)S(1)} %get-tuple-element.51), channel_id=1, source_target_pairs={{1,0},{2,1},{3,2},{4,3},{5,4},{6,5},{7,6},{9,8},{10,9},{11,10},{12... | collective-permute-start | bytes 61448 | tf_op jit(solution)/shard_map/ppermute | solution.py:25
  190.6 12.0 %collective-permute-start.31 = (f32[5,8,1,128]{3,2,0,1:T(1,128)S(1)}, f32[5,8,1,128]{3,2,0,1:T(1,128)S(1)}, u32[]{:S(2)}, u32[]{:S(2)}) collective-permute-start(f32[5,8,1,128]{3,2,0,1:T(1,128)S(1)} %get-tuple-element.60), channel_id=1, source_target_pairs={{0,8},{8,16},{16,24},{24,32},{32,40},{40,48},{48,56},{56,64},{64,7... | collective-permute-start | bytes 61448 | tf_op jit(solution)/shard_map/ppermute | solution.py:23
  192.5 10.1 %collective-permute-start.32 = (f32[5,8,1,128]{3,2,0,1:T(1,128)S(1)}, f32[5,8,1,128]{3,2,0,1:T(1,128)S(1)}, u32[]{:S(2)}, u32[]{:S(2)}) collective-permute-start(f32[5,8,1,128]{3,2,0,1:T(1,128)S(1)} %get-tuple-element.61), channel_id=1, source_target_pairs={{8,0},{16,8},{24,16},{32,24},{40,32},{48,40},{56,48},{64,56},{72,6... | collective-permute-start | bytes 61448 | tf_op jit(solution)/shard_map/ppermute | solution.py:25
  200.7 8.0 %collective-permute-start.27 = (f32[5,9,128]{2,1,0:T(8,128)S(1)}, f32[5,9,128]{2,1,0:T(8,128)S(1)}, u32[]{:S(2)}, u32[]{:S(2)}) collective-permute-start(f32[5,9,128]{2,1,0:T(8,128)S(1)} %broadcast_select_fusion.9), channel_id=1, source_target_pairs={{0,64},{8,72},{16,80},{24,88},{32,96},{40,104},{48,112},{56,120},{... | collective-permute-start | bytes 69128 | tf_op jit(solution)/shard_map/ppermute | solution.py:12
  236.6 10.1 %collective-permute-start.35 = (f32[5,9,128]{2,1,0:T(8,128)S(1)}, f32[5,9,128]{2,1,0:T(8,128)S(1)}, u32[]{:S(2)}, u32[]{:S(2)}) collective-permute-start(f32[5,9,128]{2,1,0:T(8,128)S(1)} %pad_maximum_fusion.11), channel_id=1, source_target_pairs={{0,8},{8,16},{16,24},{24,32},{32,40},{40,48},{48,56},{56,64},{64,7... | collective-permute-start | bytes 69128 | tf_op jit(solution)/shard_map/ppermute | solution.py:12
  246.7 11.0 %collective-permute-start.36 = (f32[5,9,128]{2,1,0:T(8,128)S(1)}, f32[5,9,128]{2,1,0:T(8,128)S(1)}, u32[]{:S(2)}, u32[]{:S(2)}) collective-permute-start(f32[5,9,128]{2,1,0:T(8,128)S(1)} %broadcast_select_fusion), channel_id=1, source_target_pairs={{0,16},{8,24},{16,32},{24,40},{32,48},{40,56},{48,64},{56,72},{64,... | collective-permute-start | bytes 69128 | tf_op jit(solution)/shard_map/ppermute | solution.py:12
  257.7 14.0 %collective-permute-start.37 = (f32[5,9,128]{2,1,0:T(8,128)S(1)}, f32[5,9,128]{2,1,0:T(8,128)S(1)}, u32[]{:S(2)}, u32[]{:S(2)}) collective-permute-start(f32[5,9,128]{2,1,0:T(8,128)S(1)} %broadcast_select_fusion.4), channel_id=1, source_target_pairs={{0,32},{8,40},{16,48},{24,56},{32,64},{40,72},{48,80},{56,88},{64,... | collective-permute-start | bytes 69128 | tf_op jit(solution)/shard_map/ppermute | solution.py:12
  259.7 34.8 %collective-permute-start.41 = (f32[5,1,8,128]{3,2,0,1:T(8,128)S(1)}, f32[5,1,8,128]{3,2,0,1:T(8,128)S(1)}, u32[]{:S(2)}, u32[]{:S(2)}) collective-permute-start(f32[5,1,8,128]{3,2,0,1:T(8,128)S(1)} %get-tuple-element.23), channel_id=1, source_target_pairs={{1,0},{2,1},{3,2},{4,3},{5,4},{6,5},{7,6},{9,8},{10,9},{11,10},{12... | collective-permute-start | bytes 61448 | tf_op jit(solution)/shard_map/ppermute | solution.py:25
  261.6 12.0 %collective-permute-start.42 = (f32[5,8,1,128]{3,2,0,1:T(1,128)S(1)}, f32[5,8,1,128]{3,2,0,1:T(1,128)S(1)}, u32[]{:S(2)}, u32[]{:S(2)}) collective-permute-start(f32[5,8,1,128]{3,2,0,1:T(1,128)S(1)} %get-tuple-element.32), channel_id=1, source_target_pairs={{0,8},{8,16},{16,24},{24,32},{32,40},{40,48},{48,56},{56,64},{64,7... | collective-permute-start | bytes 61448 | tf_op jit(solution)/shard_map/ppermute | solution.py:23
  263.6 10.1 %collective-permute-start.43 = (f32[5,8,1,128]{3,2,0,1:T(1,128)S(1)}, f32[5,8,1,128]{3,2,0,1:T(1,128)S(1)}, u32[]{:S(2)}, u32[]{:S(2)}) collective-permute-start(f32[5,8,1,128]{3,2,0,1:T(1,128)S(1)} %get-tuple-element.33), channel_id=1, source_target_pairs={{8,0},{16,8},{24,16},{32,24},{40,32},{48,40},{56,48},{64,56},{72,6... | collective-permute-start | bytes 61448 | tf_op jit(solution)/shard_map/ppermute | solution.py:25
  271.7 8.0 %collective-permute-start.38 = (f32[5,9,128]{2,1,0:T(8,128)S(1)}, f32[5,9,128]{2,1,0:T(8,128)S(1)}, u32[]{:S(2)}, u32[]{:S(2)}) collective-permute-start(f32[5,9,128]{2,1,0:T(8,128)S(1)} %broadcast_select_fusion.8), channel_id=1, source_target_pairs={{0,64},{8,72},{16,80},{24,88},{32,96},{40,104},{48,112},{56,120},{... | collective-permute-start | bytes 69128 | tf_op jit(solution)/shard_map/ppermute | solution.py:12
  (17 other events, 286.0 us)
where the time goes:
time: 298 us; the launch traced here: 296 us
  waiting for transfers between devices  170 us (57%)
  starting transfers between devices  115 us (39%)
  local copies, waits for them, and re-layouts  5.69 us (2%)
    ppermute x28, waiting for transfers between devices, passed_along(): return lax.ppermute(value, axis, pairs)  154 us
    ppermute x28, starting transfers between devices, passed_along(): return lax.ppermute(value, axis, pairs)  60.2 us
    ppermute x8, starting transfers between devices, padded(): lax.ppermute(head, axis, [((i + 1) % count, i) for i in range(ends)])  39.2 us
    ppermute x8, starting transfers between devices, padded(): lax.ppermute(tail, axis, [(i, (i + 1) % count) for i in range(ends)])  16 us
    ppermute x8, waiting for transfers between devices, padded(): lax.ppermute(tail, axis, [(i, (i + 1) % count) for i in range(ends)])  15.9 us
  transfers between devices with their start and end apart: 44, of which 27 were waited for; matrix products, arithmetic and copies ran while one was open for 2% of the time, Pallas kernels for 0%

commit v1 on v0

v1 whole, which is shorter than its diff:
```python
import functools

import jax
import jax.numpy as jnp
from jax import lax
from jax.experimental import pallas as pl
from jax.experimental.pallas import tpu as pltpu
from jax.sharding import PartitionSpec as P

ITERS = 4
MESH = pl.DeviceIdType.MESH
LEFT, RIGHT, DOWN, UP = range(4)


def radices(sectors):
    return (sectors // 16, 2, 8) if sectors >= 16 else (2, 2, 2)


def kernel(
    sectors,
    blocks,
    prev_ref,
    source_ref,
    faces_ref,
    inverse_ref,
    offset_ref,
    cells_ref,
    weights_ref,
    out_ref,
    update_ref,
    field,
    partial,
    source,
    faces_narrow,
    inverse_narrow,
    faces,
    inverse,
    first_columns,
    last_columns,
    from_left,
    from_right,
    from_below,
    from_above,
    slots_y,
    message_x,
    slots_x,
    message_z,
    slots_z,
    load_sems,
    send_sems,
    recv_sems,
    send_y,
    recv_y,
    send_x,
    recv_x,
    send_z,
    recv_z,
):
    layers, around, radial = prev_ref.shape[1:]
    across, deep, along = radices(sectors)
    group = deep * along
    sector = lax.axis_index("sector")
    block = lax.axis_index("block")
    at_x = sector // group
    at_z = lax.rem(sector // along, deep)
    at_y = lax.rem(sector, along)
    left = lax.rem(sector + sectors - 1, sectors)
    right = lax.rem(sector + 1, sectors)
    is_facing = block == blocks // 2 - 1
    is_faced = block == blocks // 2
    has_above = block < blocks - 1
    has_below = block > 0

    def place(x, z, y):
        return x * group + z * along + y

    def moved_y(distance):
        return place(at_x, at_z, lax.rem(at_y + distance + along, along))

    def moved_x(distance):
        return place(lax.rem(at_x + distance + across, across), at_z, at_y)

    def moved_z(distance):
        return place(at_x, lax.rem(at_z + distance + deep, deep), at_y)

    barrier = pltpu.get_barrier_semaphore()

    def greet(to_sector, to_block):
        pl.semaphore_signal(barrier, inc=1, device_id=(to_sector, to_block), device_id_type=MESH)

    @pl.when(is_faced)
    def _():
        for distance in range(deep):
            greet(moved_z(-distance), block - 1)

    @pl.when(is_facing)
    def _():
        for distance in range(1, along):
            greet(moved_y(-distance), block)
        for distance in range(1, across):
            greet(moved_x(-distance), block)

    greet(left, block)
    greet(right, block)

    @pl.when(has_above)
    def _():
        greet(sector, block + 1)

    @pl.when(jnp.logical_and(has_below, jnp.logical_not(is_faced)))
    def _():
        greet(sector, block - 1)

    def load(index, src, dst):
        return pltpu.make_async_copy(src, dst, load_sems.at[index])

    load_prev = load(0, prev_ref, field.at[0, :, pl.ds(1, layers)])
    load_source = load(1, source_ref, source)
    load_faces = load(2, faces_ref, faces_narrow)
    load_inverse = load(3, inverse_ref, inverse_narrow)
    load_prev.start()
    load_faces.start()
    load_inverse.start()
    load_source.start()

    def remote(src, dst, send_sem, recv_sem, to_sector, to_block):
        return pltpu.make_async_remote_copy(
            src_ref=src,
            dst_ref=dst,
            send_sem=send_sem,
            recv_sem=recv_sem,
            device_id=(to_sector, to_block),
            device_id_type=MESH,
        )

    def step_copy(k, direction, src, dst, to_sector, to_block):
        return remote(src, dst, send_sems.at[k, direction], recv_sems.at[k, direction], to_sector, to_block)

    def to_left(k):
        return step_copy(k, LEFT, first_columns.at[k], from_right.at[k], left, block)

    def to_right(k):
        return step_copy(k, RIGHT, last_columns.at[k], from_left.at[k], right, block)

    def downward(k):
        return step_copy(k, DOWN, field.at[k, :, 1], from_above.at[k], sector, block - 1)

    def upward(k):
        return step_copy(k, UP, field.at[k, :, layers], from_below.at[k], sector, block + 1)

    def row_y(k, distance):
        return remote(
            field.at[k, :, layers],
            slots_y.at[k, distance],
            send_y.at[k, distance],
            recv_y.at[k, distance],
            moved_y(distance),
            block,
        )

    def row_x(k, distance):
        return remote(
            message_x.at[k],
            slots_x.at[k, distance],
            send_x.at[k, distance],
            recv_x.at[k, distance],
            moved_x(distance),
            block,
        )

    def row_z(k, distance):
        return remote(
            message_z.at[k],
            slots_z.at[k, distance],
            send_z.at[k, distance],
            recv_z.at[k, distance],
            moved_z(distance),
            block + 1,
        )

    def path(offset):
        back_y = lax.rem(offset, along)
        rest = offset // along + (at_y < back_y).astype(jnp.int32)
        back_z = lax.rem(rest, deep)
        return back_y, rest // deep, back_z

    row_path = path(offset_ref[0])
    column_path = path(offset_ref[0] - 1)

    def slot_x(whole):
        _, back_x, back_z = whole
        return lax.rem(back_x + (at_z + back_z >= deep).astype(jnp.int32), across)

    nothing = jnp.zeros((5, around, radial), jnp.float32)

    def clear(k, carry):
        field[k, :, 0] = nothing
        field[k, :, layers + 1] = nothing

        @pl.when(jnp.logical_not(has_below))
        def _():
            from_below[k] = nothing

        @pl.when(jnp.logical_not(has_above))
        def _():
            from_above[k] = nothing

        @pl.when(is_facing)
        def _():
            message_x[k, 5] = jnp.zeros((around, radial), jnp.float32)

        return carry

    lax.fori_loop(0, ITERS, clear, 0)

    def masks(count):
        shape = (count, around, radial)
        rows = lax.broadcasted_iota(jnp.int32, shape, 1)
        lanes = lax.broadcasted_iota(jnp.int32, shape, 2)
        return rows == 0, rows == around - 1, lanes == 0, lanes == radial - 1

    def pack(k, some, value):
        first_columns[k, :, some] = value[:, :, 0:1]
        last_columns[k, :, some] = value[:, :, around - 1 : around]

    def send(k):
        @pl.when(is_facing)
        def _():
            for distance in range(1, along):
                row_y(k, distance).start()
            slots_y[k, 0] = field[k, :, layers]

        @pl.when(jnp.logical_and(has_above, jnp.logical_not(is_facing)))
        def _():
            upward(k).start()

        @pl.when(has_below)
        def _():
            downward(k).start()

        to_left(k).start()
        to_right(k).start()

    def pick(index, choices):
        value = choices[0]
        wanted = jnp.broadcast_to(index, value.shape)
        for place_back in range(1, len(choices)):
            value = jnp.where(wanted == place_back, choices[place_back], value)
        return value

    def turn_x(k):
        for distance in range(1, along):
            row_y(k, distance).wait_recv()
        message_x[k, pl.ds(0, 5)] = pick(row_path[0], [slots_y[k, back] for back in range(along)])
        message_x[k, 5, pl.ds(0, 5)] = pick(
            column_path[0], [slots_y[k, back, :, 0] for back in range(along)]
        )
        for distance in range(1, across):
            row_x(k, distance).start()
        slots_x[k, 0] = message_x[k]

    def turn_z(k):
        for distance in range(1, across):
            row_x(k, distance).wait_recv()
        message_z[k, pl.ds(0, 5)] = pick(
            slot_x(row_path), [slots_x[k, back, pl.ds(0, 5)] for back in range(across)]
        )
        message_z[k, 5] = pick(slot_x(column_path), [slots_x[k, back, 5] for back in range(across)])
        for distance in range(deep):
            row_z(k, distance).start()

    def receive_axial(k):
        @pl.when(has_above)
        def _():
            downward(k).wait_recv()

        @pl.when(jnp.logical_and(has_below, jnp.logical_not(is_faced)))
        def _():
            upward(k).wait_recv()

        @pl.when(is_faced)
        def _():
            for distance in range(deep):
                row_z(k, distance).wait_recv()
            blend_facing(k)

    def blend_facing(k):
        rows = lax.broadcasted_iota(jnp.int32, (around, radial), 0)
        donors = jnp.zeros((around, radial), jnp.int32)
        shares = jnp.zeros((around, radial), jnp.float32)
        for cell in range(around):
            donors = jnp.where(rows == cell, cells_ref[cell], donors)
            shares = jnp.where(rows == cell, weights_ref[cell], shares)
        facing = pick(row_path[2], [slots_z[k, back, pl.ds(0, 5)] for back in range(deep)])
        extra = pick(column_path[2], [slots_z[k, back, 5] for back in range(deep)])
        blended = nothing
        for column in range(around + 1):
            share = jnp.where(donors == column, shares, jnp.where(donors == column - 1, 1.0 - shares, 0.0))
            if column < around:
                row = facing[:, column : column + 1]
            else:
                row = jnp.stack([extra[comp : comp + 1] for comp in range(5)])
            blended = blended + share[None] * jnp.broadcast_to(row, (5, around, radial))
        from_below[k] = blended

    def begin(k, low, count):
        some = pl.ds(low, count)
        top, bottom, hub, shroud = masks(count)
        total = source[:, some]
        for comp in range(5):
            here = field[k, comp, pl.ds(low + 1, count)]
            mixed = (
                0.6 * field[k, comp, some] + 0.4 * field[k, comp, pl.ds(low + 2, count)],
                0.6 * jnp.where(top, 0.0, pltpu.roll(here, 1, 1))
                + 0.4 * jnp.where(bottom, 0.0, pltpu.roll(here, around - 1, 1)),
                0.6 * jnp.where(hub, 0.0, pltpu.roll(here, 1, 2))
                + 0.4 * jnp.where(shroud, 0.0, pltpu.roll(here, radial - 1, 2)),
            )
            for direction in range(3):
                total = total + faces[direction, comp, :, some] * mixed[direction][None]
        partial[:, some] = total

    def add_axial(k, layer, share, halo):
        total = partial[:, layer]
        for comp in range(5):
            total = total + faces[0, comp, :, layer] * (share * halo[k, comp])[None]
        partial[:, layer] = total

    def finish(k, low, count):
        some = pl.ds(low, count)
        top, bottom, _, _ = masks(count)
        total = partial[:, some]
        for comp in range(5):
            behind = jnp.broadcast_to(0.6 * from_left[k, comp, some], (count, around, radial))
            ahead = jnp.broadcast_to(0.4 * from_right[k, comp, some], (count, around, radial))
            mixed = jnp.where(top, behind, jnp.where(bottom, ahead, 0.0))
            total = total + faces[1, comp, :, some] * mixed[None]
        value = inverse[0, :, some] * total[0][None]
        for comp in range(1, 5):
            value = value + inverse[comp, :, some] * total[comp][None]
        field[k + 1, :, pl.ds(low + 1, count)] = value
        pack(k + 1, some, value)

    load_prev.wait()
    pack(0, pl.ds(0, layers), field[0, :, pl.ds(1, layers)])

    ends = jnp.logical_or(block == 0, block == blocks - 1)
    ends_extra = 0 if blocks > 2 else -1

    @pl.when(is_facing)
    def _():
        pl.semaphore_wait(barrier, 3 + ends_extra + (along - 1) + (across - 1) + deep)

    @pl.when(jnp.logical_and(ends, jnp.logical_not(is_facing)))
    def _():
        pl.semaphore_wait(barrier, 3)

    @pl.when(jnp.logical_not(jnp.logical_or(ends, is_facing)))
    def _():
        pl.semaphore_wait(barrier, 4)

    half = layers // 2
    inner = half - 1

    def widen_faces(index, carry):
        direction, comp = index // 5, lax.rem(index, 5)
        faces[direction, comp] = faces_narrow[direction, comp].astype(jnp.float32)
        return carry

    def widen_inverse(index, carry):
        onto, comp = index // 5, lax.rem(index, 5)
        inverse[comp, onto] = inverse_narrow[onto, comp].astype(jnp.float32)
        return carry

    def sweep(k, carry):
        send(k)

        @pl.when(k == 0)
        def _():
            load_faces.wait()
            load_inverse.wait()
            lax.fori_loop(0, 15, widen_faces, 0)
            lax.fori_loop(0, 25, widen_inverse, 0)
            load_source.wait()

        @pl.when(jnp.logical_and(is_facing, lax.rem(k, 2) == 1))
        def _():
            turn_x(k - 1)
            turn_x(k)
            turn_z(k - 1)
            turn_z(k)

        begin(k, 0, half)
        begin(k, half, half)
        to_left(k).wait_recv()
        to_right(k).wait_recv()
        finish(k, 1, inner)
        finish(k, half, inner)
        receive_axial(k)
        add_axial(k, 0, 0.6, from_below)
        add_axial(k, layers - 1, 0.4, from_above)
        finish(k, 0, 1)
        finish(k, layers - 1, 1)
        return carry

    lax.fori_loop(0, ITERS, sweep, 0)
    result = field[ITERS, :, pl.ds(1, layers)]
    out_ref[...] = result
    update_ref[...] = result - field[ITERS - 1, :, pl.ds(1, layers)]

    def settle(k, carry):
        to_left(k).wait_send()
        to_right(k).wait_send()

        @pl.when(has_below)
        def _():
            downward(k).wait_send()

        @pl.when(jnp.logical_and(has_above, jnp.logical_not(is_facing)))
        def _():
            upward(k).wait_send()

        @pl.when(is_facing)
        def _():
            for distance in range(1, along):
                row_y(k, distance).wait_send()
            for distance in range(1, across):
                row_x(k, distance).wait_send()
            for distance in range(deep):
                row_z(k, distance).wait_send()

        return carry

    lax.fori_loop(0, ITERS, settle, 0)


def swept(sectors, blocks, *args):
    layers, around, radial = args[0].shape[1:]
    across, deep, along = radices(sectors)
    f32 = jnp.float32
    cells = (5, layers, around, radial)
    anywhere = pl.BlockSpec(memory_space=pl.ANY)
    scalars = pl.BlockSpec(memory_space=pltpu.SMEM)
    vmem = pl.BlockSpec(memory_space=pltpu.VMEM)
    dma = pltpu.SemaphoreType.DMA
    return pl.pallas_call(
        functools.partial(kernel, sectors, blocks),
        out_shape=[OUT(cells, f32)] * 2,
        in_specs=[anywhere] * 4 + [scalars] * 3,
        out_specs=[vmem] * 2,
        scratch_shapes=[
            pltpu.VMEM((ITERS + 1, 5, layers + 2, around, radial), f32),
            pltpu.VMEM(cells, f32),
            pltpu.VMEM(cells, f32),
            pltpu.VMEM((3, 5, 5, layers, around, radial), jnp.bfloat16),
            pltpu.VMEM((5, 5, layers, around, radial), jnp.bfloat16),
            pltpu.VMEM((3, 5, 5, layers, around, radial), f32),
            pltpu.VMEM((5, 5, layers, around, radial), f32),
            pltpu.VMEM((ITERS + 1, 5, layers, 1, radial), f32),
            pltpu.VMEM((ITERS + 1, 5, layers, 1, radial), f32),
            pltpu.VMEM((ITERS, 5, layers, 1, radial), f32),
            pltpu.VMEM((ITERS, 5, layers, 1, radial), f32),
            pltpu.VMEM((ITERS, 5, around, radial), f32),
            pltpu.VMEM((ITERS, 5, around, radial), f32),
            pltpu.VMEM((ITERS, along, 5, around, radial), f32),
            pltpu.VMEM((ITERS, 6, around, radial), f32),
            pltpu.VMEM((ITERS, across, 6, around, radial), f32),
            pltpu.VMEM((ITERS, 6, around, radial), f32),
            pltpu.VMEM((ITERS, deep, 6, around, radial), f32),
            dma((4,)),
            dma((ITERS, 4)),
            dma((ITERS, 4)),
            dma((ITERS, along)),
            dma((ITERS, along)),
            dma((ITERS, across)),
            dma((ITERS, across)),
            dma((ITERS, deep)),
            dma((ITERS, deep)),
        ],
        compiler_params=pltpu.CompilerParams(collective_id=0, has_side_effects=True),
        name="sweeps",
    )(*args)


OUT = pltpu.VMEM


def put_kernel(first_ref, second_ref, first_out, second_out, sems):
    copies = (
        pltpu.make_async_copy(first_ref, first_out, sems.at[0]),
        pltpu.make_async_copy(second_ref, second_out, sems.at[1]),
    )
    for copy in copies:
        copy.start()
    for copy in copies:
        copy.wait()


def put(*values):
    anywhere = pl.BlockSpec(memory_space=pl.ANY)
    return pl.pallas_call(
        put_kernel,
        out_shape=[jax.ShapeDtypeStruct(value.shape, value.dtype) for value in values],
        in_specs=[anywhere] * 2,
        out_specs=[anywhere] * 2,
        scratch_shapes=[pltpu.SemaphoreType.DMA((2,))],
        name="put",
    )(*values)


def shards(prev, source, faces, inverse, sector_offset, donor_cells, donor_weights):
    result = swept(
        lax.axis_size("sector"),
        lax.axis_size("block"),
        prev,
        source,
        faces,
        inverse,
        sector_offset,
        donor_cells,
        donor_weights,
    )
    return tuple(result)


def solution(mesh):
    return jax.shard_map(
        shards,
        mesh=mesh,
        in_specs=(
            P(None, "block", "sector", None),
            P(None, "block", "sector", None),
            P(None, None, None, "block", "sector", None),
            P(None, None, "block", "sector", None),
            P(),
            P("sector"),
            P("sector"),
        ),
        out_specs=(P(None, "block", "sector", None), P(None, "block", "sector", None)),
        check_vma=False,
    )
```

time: 298 us -> 48.2 us (0.16)
  the two profiles are of different devices: /device:TPU:256 before, /device:TPU:129 now
where the time goes in v1:
time: 48.2 us; the launch traced here: 48.1 us
  Pallas kernels  45.5 us (94%)
  local copies, waits for them, and re-layouts  1.33 us (3%)
  between operations  1.29 us (3%)
    pallas_call x1, Pallas kernels, swept(): pl.pallas_call(functools.partial(kernel, sectors, blocks), out_shape=[OUT...  45.5 us
    unnamed x2, local copies, waits for them, and re-layouts  1.33 us

profile of v1, /device:TPU:129, one launch (start us, length us, event | category | flops | bytes accessed | tf_op | source)
XLA Modules:
  0.0 48.1 jit_solution(8344204648636758858)
XLA Ops:
  1.3 45.5 %sweeps.1 = (f32[5,8,8,128]{3,2,1,0:T(8,128)S(1)}, f32[5,8,8,128]{3,2,1,0:T(8,128)S(1)}) custom-call(f32[5,8,8,128]{3,2,1,0:T(8,128)} %prev_ref.1, f32[5,8,8,128]{3,2,1,0:T(8,128)} %source_ref.1, bf16[3,5,5,8,8,128]{5,4,3,2,1,0:T(8,128)(2,1)} %faces_ref.1, bf16[5,5,8,8,128]{4,3,2,1,0:T(8,128)(2,1)} %inverse_ref.1, s32[1]{0:T(128)S(6)} %copy.13.offset_ref, ...), custom_call_target="tpu_custom_call" | custom-call | tf_op jit(solution)/shard_map/sweeps/pallas_call | solution.py:446
  46.7 0.7 %copy.11 = f32[5,8,8,128]{3,2,1,0:T(8,128)} copy(f32[5,8,8,128]{3,2,1,0:T(8,128)S(1)} %get-tuple-element.2) | data formatting | bytes 327680
  47.4 0.7 %copy.12 = f32[5,8,8,128]{3,2,1,0:T(8,128)} copy(f32[5,8,8,128]{3,2,1,0:T(8,128)S(1)} %get-tuple-element.3) | data formatting | bytes 327680

commit v2 on v1

--- a/solution.py
+++ b/solution.py
@@ -224,22 +224,22 @@
         last_columns[k, :, some] = value[:, :, around - 1 : around]
 
     def send(k):
+        to_left(k).start()
+        to_right(k).start()
+
+        @pl.when(has_below)
+        def _():
+            downward(k).start()
+
+        @pl.when(jnp.logical_and(has_above, jnp.logical_not(is_facing)))
+        def _():
+            upward(k).start()
+
         @pl.when(is_facing)
         def _():
-            for distance in range(1, along):
+            for distance in sorted(range(1, along), key=lambda d: -min(d, along - d)):
                 row_y(k, distance).start()
             slots_y[k, 0] = field[k, :, layers]
-
-        @pl.when(jnp.logical_and(has_above, jnp.logical_not(is_facing)))
-        def _():
-            upward(k).start()
-
-        @pl.when(has_below)
-        def _():
-            downward(k).start()
-
-        to_left(k).start()
-        to_right(k).start()
 
     def pick(index, choices):
         value = choices[0]
@@ -255,7 +255,7 @@
         message_x[k, 5, pl.ds(0, 5)] = pick(
             column_path[0], [slots_y[k, back, :, 0] for back in range(along)]
         )
-        for distance in range(1, across):
+        for distance in sorted(range(1, across), key=lambda d: -min(d, across - d)):
             row_x(k, distance).start()
         slots_x[k, 0] = message_x[k]
 
@@ -385,10 +385,9 @@
 
         @pl.when(jnp.logical_and(is_facing, lax.rem(k, 2) == 1))
         def _():
-            turn_x(k - 1)
-            turn_x(k)
-            turn_z(k - 1)
-            turn_z(k)
+            for earlier in (1, 0):
+                turn_x(k - earlier)
+                turn_z(k - earlier)
 
         begin(k, 0, half)
         begin(k, half, half)

time: 48.2 us -> 45.8 us (0.950)
  Pallas kernels: 45.5 us -> 43.1 us
    pallas_call x1, Pallas kernels: 45.5 us -> 43.1 us  [swept(): pl.pallas_call(functools.partial(kernel, sectors, blocks), out_shape=[OUT...]
where the time goes in v2:
time: 45.8 us; the launch traced here: 45.7 us
  Pallas kernels  43.1 us (94%)
  local copies, waits for them, and re-layouts  1.33 us (3%)
  between operations  1.29 us (3%)
    pallas_call x1, Pallas kernels, swept(): pl.pallas_call(functools.partial(kernel, sectors, blocks), out_shape=[OUT...  43.1 us
    unnamed x2, local copies, waits for them, and re-layouts  1.33 us

profile of v2, /device:TPU:129, one launch (start us, length us, event | category | flops | bytes accessed | tf_op | source)
XLA Modules:
  0.0 45.7 jit_solution(13826868803500219241)
XLA Ops:
  1.3 43.1 %sweeps.1 = (f32[5,8,8,128]{3,2,1,0:T(8,128)S(1)}, f32[5,8,8,128]{3,2,1,0:T(8,128)S(1)}) custom-call(f32[5,8,8,128]{3,2,1,0:T(8,128)} %prev_ref.1, f32[5,8,8,128]{3,2,1,0:T(8,128)} %source_ref.1, bf16[3,5,5,8,8,128]{5,4,3,2,1,0:T(8,128)(2,1)} %faces_ref.1, bf16[5,5,8,8,128]{4,3,2,1,0:T(8,128)(2,1)} %inverse_ref.1, s32[1]{0:T(128)S(6)} %copy.13.offset_ref, ...), custom_call_target="tpu_custom_call" | custom-call | tf_op jit(solution)/shard_map/sweeps/pallas_call | solution.py:445
  44.3 0.7 %copy.11 = f32[5,8,8,128]{3,2,1,0:T(8,128)} copy(f32[5,8,8,128]{3,2,1,0:T(8,128)S(1)} %get-tuple-element.2) | data formatting | bytes 327680
  45.0 0.7 %copy.12 = f32[5,8,8,128]{3,2,1,0:T(8,128)} copy(f32[5,8,8,128]{3,2,1,0:T(8,128)S(1)} %get-tuple-element.3) | data formatting | bytes 327680

commit v3 on v2

--- a/solution.py
+++ b/solution.py
@@ -17,6 +17,7 @@
 
 
 def kernel(
+    turn,
     sectors,
     blocks,
     prev_ref,
@@ -42,6 +43,7 @@
     from_below,
     from_above,
     slots_y,
+    slots_c,
     message_x,
     slots_x,
     message_z,
@@ -59,6 +61,7 @@
     layers, around, radial = prev_ref.shape[1:]
     across, deep, along = radices(sectors)
     group = deep * along
+    column_turn = (turn - 1) % along
     sector = lax.axis_index("sector")
     block = lax.axis_index("block")
     at_x = sector // group
@@ -95,8 +98,9 @@
 
     @pl.when(is_facing)
     def _():
-        for distance in range(1, along):
-            greet(moved_y(-distance), block)
+        for distance in (turn, column_turn):
+            if distance:
+                greet(moved_y(-distance), block)
         for distance in range(1, across):
             greet(moved_x(-distance), block)
 
@@ -148,13 +152,18 @@
     def upward(k):
         return step_copy(k, UP, field.at[k, :, layers], from_below.at[k], sector, block + 1)
 
-    def row_y(k, distance):
+    def row_y(k):
         return remote(
-            field.at[k, :, layers],
-            slots_y.at[k, distance],
-            send_y.at[k, distance],
-            recv_y.at[k, distance],
-            moved_y(distance),
+            field.at[k, :, layers], slots_y.at[k], send_y.at[k, 0], recv_y.at[k, 0], moved_y(turn), block
+        )
+
+    def column_y(k):
+        return remote(
+            first_columns.at[k, :, layers - 1],
+            slots_c.at[k],
+            send_y.at[k, 1],
+            recv_y.at[k, 1],
+            moved_y(column_turn),
             block,
         )
 
@@ -237,9 +246,10 @@
 
         @pl.when(is_facing)
         def _():
-            for distance in sorted(range(1, along), key=lambda d: -min(d, along - d)):
-                row_y(k, distance).start()
-            slots_y[k, 0] = field[k, :, layers]
+            if turn:
+                row_y(k).start()
+            if column_turn:
+                column_y(k).start()
 
     def pick(index, choices):
         value = choices[0]
@@ -249,12 +259,16 @@
         return value
 
     def turn_x(k):
-        for distance in range(1, along):
-            row_y(k, distance).wait_recv()
-        message_x[k, pl.ds(0, 5)] = pick(row_path[0], [slots_y[k, back] for back in range(along)])
-        message_x[k, 5, pl.ds(0, 5)] = pick(
-            column_path[0], [slots_y[k, back, :, 0] for back in range(along)]
-        )
+        if turn:
+            row_y(k).wait_recv()
+            message_x[k, pl.ds(0, 5)] = slots_y[k]
+        else:
+            message_x[k, pl.ds(0, 5)] = field[k, :, layers]
+        if column_turn:
+            column_y(k).wait_recv()
+            message_x[k, 5, pl.ds(0, 5)] = slots_c[k, :, 0]
+        else:
+            message_x[k, 5, pl.ds(0, 5)] = field[k, :, layers, 0]
         for distance in sorted(range(1, across), key=lambda d: -min(d, across - d)):
             row_x(k, distance).start()
         slots_x[k, 0] = message_x[k]
@@ -349,7 +363,7 @@
 
     @pl.when(is_facing)
     def _():
-        pl.semaphore_wait(barrier, 3 + ends_extra + (along - 1) + (across - 1) + deep)
+        pl.semaphore_wait(barrier, 3 + ends_extra + bool(turn) + bool(column_turn) + (across - 1) + deep)
 
     @pl.when(jnp.logical_and(ends, jnp.logical_not(is_facing)))
     def _():
@@ -421,8 +435,10 @@
 
         @pl.when(is_facing)
         def _():
-            for distance in range(1, along):
-                row_y(k, distance).wait_send()
+            if turn:
+                row_y(k).wait_send()
+            if column_turn:
+                column_y(k).wait_send()
             for distance in range(1, across):
                 row_x(k, distance).wait_send()
             for distance in range(deep):
@@ -433,7 +449,7 @@
     lax.fori_loop(0, ITERS, settle, 0)
 
 
-def swept(sectors, blocks, *args):
+def swept(turn, sectors, blocks, *args):
     layers, around, radial = args[0].shape[1:]
     across, deep, along = radices(sectors)
     f32 = jnp.float32
@@ -443,7 +459,7 @@
     vmem = pl.BlockSpec(memory_space=pltpu.VMEM)
     dma = pltpu.SemaphoreType.DMA
     return pl.pallas_call(
-        functools.partial(kernel, sectors, blocks),
+        functools.partial(kernel, turn, sectors, blocks),
         out_shape=[OUT(cells, f32)] * 2,
         in_specs=[anywhere] * 4 + [scalars] * 3,
         out_specs=[vmem] * 2,
@@ -461,7 +477,8 @@
             pltpu.VMEM((ITERS, 5, layers, 1, radial), f32),
             pltpu.VMEM((ITERS, 5, around, radial), f32),
             pltpu.VMEM((ITERS, 5, around, radial), f32),
-            pltpu.VMEM((ITERS, along, 5, around, radial), f32),
+            pltpu.VMEM((ITERS, 5, around, radial), f32),
+            pltpu.VMEM((ITERS, 5, 1, radial), f32),
             pltpu.VMEM((ITERS, 6, around, radial), f32),
             pltpu.VMEM((ITERS, across, 6, around, radial), f32),
             pltpu.VMEM((ITERS, 6, around, radial), f32),
@@ -469,14 +486,14 @@
             dma((4,)),
             dma((ITERS, 4)),
             dma((ITERS, 4)),
-            dma((ITERS, along)),
-            dma((ITERS, along)),
+            dma((ITERS, 2)),
+            dma((ITERS, 2)),
             dma((ITERS, across)),
             dma((ITERS, across)),
             dma((ITERS, deep)),
             dma((ITERS, deep)),
         ],
-        compiler_params=pltpu.CompilerParams(collective_id=0, has_side_effects=True),
+        compiler_params=pltpu.CompilerParams(collective_id=turn, has_side_effects=True),
         name="sweeps",
     )(*args)
 
@@ -508,9 +525,12 @@
 
 
 def shards(prev, source, faces, inverse, sector_offset, donor_cells, donor_weights):
-    result = swept(
-        lax.axis_size("sector"),
-        lax.axis_size("block"),
+    sectors = lax.axis_size("sector")
+    along = radices(sectors)[2]
+    branches = [functools.partial(swept, turn, sectors, lax.axis_size("block")) for turn in range(along)]
+    result = lax.switch(
+        lax.rem(sector_offset[0], along),
+        branches,
         prev,
         source,
         faces,

time: 45.8 us -> 45.1 us (0.985)
  Pallas kernels: 43.1 us -> 42.3 us
    pallas_call x1, Pallas kernels: 43.1 us -> 42.3 us  [swept(): pl.pallas_call(functools.partial(kernel, turn, sectors, blocks), out_shap...]
where the time goes in v3:
time: 45.1 us; the launch traced here: 45 us
  Pallas kernels  42.3 us (94%)
  local copies, waits for them, and re-layouts  1.33 us (3%)
  between operations  1.29 us (3%)
    pallas_call x1, Pallas kernels, swept(): pl.pallas_call(functools.partial(kernel, turn, sectors, blocks), out_shap...  42.3 us
    unnamed x2, local copies, waits for them, and re-layouts  1.33 us

profile of v3, /device:TPU:129, one launch (start us, length us, event | category | flops | bytes accessed | tf_op | source)
XLA Modules:
  0.0 45.0 jit_solution(2618212110643341184)
XLA Ops:
  1.3 42.3 %conditional.1 = ((f32[5,8,8,128]{3,2,1,0:T(8,128)S(1)}, f32[5,8,8,128]{3,2,1,0:T(8,128)S(1)})) conditional(s32[]{:T(128)} %clamp.3, (f32[5,8,8,128]{3,2,1,0:T(8,128)}, f32[5,8,8,128]{3,2,1,0:T(8,128)}, bf16[3,5,5,8,8,128]{5,4,3,2,1,0:T(8,128)(2,1)}, bf16[5,5,8,8,128]{4,3,2,1,0:T(8,128)(2,1)}, s32[1]{0:T(128)}, ...), branch_computations={%region_0.0_spmd, %region_1.0_spmd, %region_2.0_spmd, %region_3.0_... | conditional | bytes 8 | solution.py:531
  1.3 42.3 %sweeps.12 = (f32[5,8,8,128]{3,2,1,0:T(8,128)S(1)}, f32[5,8,8,128]{3,2,1,0:T(8,128)S(1)}) custom-call(f32[5,8,8,128]{3,2,1,0:T(8,128)} %get-tuple-element.140.prev_ref, f32[5,8,8,128]{3,2,1,0:T(8,128)} %get-tuple-element.141.source_ref, bf16[3,5,5,8,8,128]{5,4,3,2,1,0:T(8,128)(2,1)} %get-tuple-element.142.faces_ref, ...), custom_call_target="tpu_custom_call" | custom-call | tf_op jit(solution)/shard_map/cond/branch_4_fun/sweeps/pallas_call | solution.py:461
  43.6 0.7 %copy.43 = f32[5,8,8,128]{3,2,1,0:T(8,128)} copy(f32[5,8,8,128]{3,2,1,0:T(8,128)S(1)} %get-tuple-element.204) | data formatting | bytes 327680
  44.3 0.7 %copy.44 = f32[5,8,8,128]{3,2,1,0:T(8,128)} copy(f32[5,8,8,128]{3,2,1,0:T(8,128)S(1)} %get-tuple-element.205) | data formatting | bytes 327680

commit v4 on v3

--- a/solution.py
+++ b/solution.py
@@ -399,12 +399,21 @@
 
         @pl.when(jnp.logical_and(is_facing, lax.rem(k, 2) == 1))
         def _():
-            for earlier in (1, 0):
-                turn_x(k - earlier)
-                turn_z(k - earlier)
+            @pl.when(k > 1)
+            def _():
+                turn_x(k - 1)
+
+            turn_z(k - 1)
+            turn_x(k)
+            turn_z(k)
 
         begin(k, 0, half)
         begin(k, half, half)
+
+        @pl.when(jnp.logical_and(is_facing, k == 0))
+        def _():
+            turn_x(0)
+
         to_left(k).wait_recv()
         to_right(k).wait_recv()
         finish(k, 1, inner)

time: 45.1 us -> 44.3 us (0.982); the launches traced: 45 us -> 43.6 us
  Pallas kernels: 42.3 us -> 41 us
    pallas_call x1, Pallas kernels: 42.3 us -> 41 us  [swept(): pl.pallas_call(functools.partial(kernel, turn, sectors, blocks), out_shap...]
where the time goes in v4:
time: 44.3 us; the launch traced here: 43.6 us
  Pallas kernels  41 us (93%)
  local copies, waits for them, and re-layouts  1.33 us (3%)
  between operations  1.29 us (3%)
    pallas_call x1, Pallas kernels, swept(): pl.pallas_call(functools.partial(kernel, turn, sectors, blocks), out_shap...  41 us
    unnamed x2, local copies, waits for them, and re-layouts  1.33 us

profile of v4, /device:TPU:129, one launch (start us, length us, event | category | flops | bytes accessed | tf_op | source)
XLA Modules:
  0.0 43.6 jit_solution(1633257875573031897)
XLA Ops:
  1.3 41.0 %conditional.1 = ((f32[5,8,8,128]{3,2,1,0:T(8,128)S(1)}, f32[5,8,8,128]{3,2,1,0:T(8,128)S(1)})) conditional(s32[]{:T(128)} %clamp.3, (f32[5,8,8,128]{3,2,1,0:T(8,128)}, f32[5,8,8,128]{3,2,1,0:T(8,128)}, bf16[3,5,5,8,8,128]{5,4,3,2,1,0:T(8,128)(2,1)}, bf16[5,5,8,8,128]{4,3,2,1,0:T(8,128)(2,1)}, s32[1]{0:T(128)}, ...), branch_computations={%region_0.0_spmd, %region_1.0_spmd, %region_2.0_spmd, %region_3.0_... | conditional | bytes 8 | solution.py:540
  1.3 41.0 %sweeps.10 = (f32[5,8,8,128]{3,2,1,0:T(8,128)S(1)}, f32[5,8,8,128]{3,2,1,0:T(8,128)S(1)}) custom-call(f32[5,8,8,128]{3,2,1,0:T(8,128)} %get-tuple-element.126.prev_ref, f32[5,8,8,128]{3,2,1,0:T(8,128)} %get-tuple-element.127.source_ref, bf16[3,5,5,8,8,128]{5,4,3,2,1,0:T(8,128)(2,1)} %get-tuple-element.128.faces_ref, ...), custom_call_target="tpu_custom_call" | custom-call | tf_op jit(solution)/shard_map/cond/branch_2_fun/sweeps/pallas_call | solution.py:470
  42.3 0.7 %copy.43 = f32[5,8,8,128]{3,2,1,0:T(8,128)} copy(f32[5,8,8,128]{3,2,1,0:T(8,128)S(1)} %get-tuple-element.204) | data formatting | bytes 327680
  43.0 0.7 %copy.44 = f32[5,8,8,128]{3,2,1,0:T(8,128)} copy(f32[5,8,8,128]{3,2,1,0:T(8,128)S(1)} %get-tuple-element.205) | data formatting | bytes 327680
